TPU v7x, 512 devices: a 4x2x32 block of a 4x8x32 slice. The times are simulated.
512 devices in a mesh: parts: 2 (over y), seq: 32 (over z), head: 8 (over x, core).
Axes of the slice: x: 4, y: 2, z: 32, core: 2. Of those that a mesh axis runs over, the one named last changes fastest.
The devices are a block of a 4x8x32 slice.
Arguments:
- hidden: bfloat16 [48, 12288], P(('parts', 'head'), 'seq'), parts along dimension 0, may hold values from -600 to 600
- norm_gain: float32 [12288], P('seq'), may hold values from 0.1 to 1.9
- w_query: bfloat16 [12288, 12288], P('seq', 'head'), may hold values from -0.0546875 to 0.0546875
- w_key: bfloat16 [12288, 1024], P('seq', 'head'), may hold values from -0.0546875 to 0.0546875
- w_value: bfloat16 [12288, 1024], P('seq', 'head'), may hold values from -0.0546875 to 0.0546875
- w_out: bfloat16 [12288, 12288], P('head', 'seq'), may hold values from -0.0546875 to 0.0546875
- lengths: int32 [48], P('parts'), parts along dimension 0, may hold values from 1 to 4096, as said below
- key_cache: bfloat16 [48, 8, 4096, 128], P('parts', 'head', 'seq'), parts along dimension 0, may hold values from -600 to 600, as said below
- value_cache: bfloat16 [48, 8, 4096, 128], P('parts', 'head', 'seq'), parts along dimension 0, may hold values from -6 to 6
Outputs:
- attn_out: bfloat16 [48, 12288], P(('parts', 'head'), 'seq'), parts along dimension 0
There are 2 independent parts, one for each index of `parts`. A program takes and returns all parts, laid end to end along the dimension named above; an argument that names none is the same for every part. Nothing has to cross between parts.
Inputs may be any that keep to these rules, and one draw needn't show every extreme that they name: Sequence b holds lengths[b] cached tokens at positions 0 to lengths[b] - 1; its new token takes position lengths[b]. `key_cache`: positions at or past a sequence's length hold no data.
All inputs are finite; a program needn't handle non-finite values.
Results may differ from a plain program's by a relative error of at most 0.0075.
The roundings to bfloat16 on the way count: a program that leaves them out, or rounds other values in their place, can miss the bound.
Values may be sent and summed in bfloat16 or wider, within the bound.
No kernel may reach another device: no remote copies, remote signals or barrier semaphores. Data moves between devices by JAX's collectives and lax.ppermute only.
A program may use at most 64 MiB of HBM per device.

v0:
```python
import math
import jax
import jax.numpy as jnp
from jax import lax
from jax.sharding import PartitionSpec as P

D = 12288
EPSILON = 1e-05


def in_order(tiles, dim):
    tiles = jnp.moveaxis(tiles, 0, dim)
    dims = tiles.shape
    return tiles.reshape(*dims[:dim], dims[dim] * dims[dim + 1], *dims[dim + 2 :])


def sent_to_all(x, axis):
    copies = jnp.broadcast_to(x, (lax.axis_size(axis), *x.shape))
    return lax.all_to_all(copies, axis, split_axis=0, concat_axis=0, tiled=True)


def gather_directly(x, axis, dim):
    return in_order(sent_to_all(x, axis), dim)


def cut_along(x, dim, peers):
    before, after = (x.shape[:dim], x.shape[dim + 1 :])
    return jnp.moveaxis(x.reshape(*before, peers, -1, *after), dim, 0)


def summed_on_arrival(x, axis, dim):
    tiles = cut_along(x, dim, lax.axis_size(axis))
    arrived = lax.all_to_all(tiles, axis, split_axis=0, concat_axis=0, tiled=True)
    return arrived.sum(axis=0)


def in_one_piece(arrays, axis, dim, along):
    ends, at = ([], 0)
    for a in arrays[:-1]:
        at += a.shape[along]
        ends.append(at)
    both = jnp.concatenate(arrays, axis=along)
    return tuple(jnp.split(summed_on_arrival(both, axis, dim), ends, axis=along))


def in_one_piece_2(arrays, axis, dim, along):
    ends, at = ([], 0)
    for a in arrays[:-1]:
        at += a.shape[along]
        ends.append(at)
    both = jnp.concatenate(arrays, axis=along)
    return tuple(jnp.split(lax.all_gather(both, axis, axis=dim, tiled=True), ends, axis=along))


def side_by_side(arrays, axis, dim, along):
    widths = [math.prod(a.shape[along:]) for a in arrays]
    both = jnp.concatenate(
        [a.reshape(*a.shape[:along], w) for a, w in zip(arrays, widths)], axis=along
    )
    result = lax.all_gather(both, axis, axis=dim, tiled=True)
    tiles = jnp.split(result, [sum(widths[:k]) for k in range(1, len(widths))], axis=along)
    return tuple(
        (b.reshape(*result.shape[:along], *a.shape[along:]) for a, b in zip(arrays, tiles))
    )


def fold_blocks(totals, pieces):
    new_max = jnp.maximum(totals[0], jnp.max(pieces[0], axis=0))
    piece_factor = jnp.exp(pieces[0] - new_max[None])
    den_total = jnp.sum(piece_factor * pieces[1], axis=0)
    acc_total = jnp.sum(piece_factor[..., None] * pieces[2], axis=0)
    return (new_max, den_total, acc_total)


def local(hidden, norm_gain, w_query, w_key, w_value, w_out, lengths, key_cache, value_cache):
    batch_size, kv_local, block_len, head_size = key_cache.shape
    group_size = w_query.shape[1] // (kv_local * head_size)
    token_rows = gather_directly(hidden, "head", 0)
    widened = token_rows.astype(jnp.float32)
    square_local = jnp.sum(widened * widened, axis=1)
    scaled = (widened * norm_gain).astype(jnp.bfloat16)
    query_part = jnp.dot(scaled, w_query, preferred_element_type=jnp.float32)
    key_part = jnp.dot(scaled, w_key, preferred_element_type=jnp.float32)
    value_part = jnp.dot(scaled, w_value, preferred_element_type=jnp.float32)
    query_factor = float(head_size) ** (-0.5)
    square_tiled = jnp.broadcast_to(square_local[:, None], (batch_size, lax.axis_size("seq")))
    query_sum, key_sum, value_sum, norm_column = (
        summed_on_arrival(query_part, "seq", 1),
        *in_one_piece((key_part, value_part), "seq", 1, 0),
        summed_on_arrival(square_tiled, "seq", 1),
    )
    norm_total = norm_column[:, 0]
    inverse_rms = lax.rsqrt(norm_total / D + EPSILON)[:, None]
    queries = (query_sum * inverse_rms * query_factor).astype(jnp.bfloat16)
    new_keys = (key_sum * inverse_rms).astype(jnp.bfloat16)
    new_values = (value_sum * inverse_rms).astype(jnp.bfloat16)
    queries, new_keys, new_values = (
        lax.all_gather(queries, "seq", axis=1, tiled=True),
        *in_one_piece_2((new_keys, new_values), "seq", 1, 0),
    )
    grouped = queries.reshape(batch_size, kv_local, group_size, head_size)
    scores = jnp.einsum("bkgd,bkpd->bkgp", grouped, key_cache, preferred_element_type=jnp.float32)
    offset = lax.axis_index("seq") * block_len
    positions = offset + jnp.arange(block_len, dtype=jnp.int32)
    live_mask = (positions[None, :] < lengths[:, None])[:, None, None, :]
    block_max = jnp.max(jnp.where(live_mask, scores, -1e30), axis=-1)
    shifted = jnp.where(live_mask, scores - block_max[..., None], 0.0)
    weights = jnp.where(live_mask, jnp.exp(shifted), 0.0).astype(jnp.bfloat16)
    block_den = jnp.sum(weights.astype(jnp.float32), axis=-1)
    block_acc = jnp.einsum(
        "bkgp,bkpd->bkgd", weights, value_cache, preferred_element_type=jnp.float32
    )
    self_score = jnp.einsum(
        "oips,ois->oip",
        grouped,
        new_keys.reshape(batch_size, kv_local, head_size),
        preferred_element_type=jnp.float32,
    )
    initial = (
        jnp.full(block_max.shape, -1e30, jnp.float32),
        jnp.zeros(block_den.shape, jnp.float32),
        jnp.zeros(block_acc.shape, jnp.float32),
    )
    global_max, den_merged, acc_merged = fold_blocks(
        initial, side_by_side((block_max[None], block_den[None], block_acc[None]), "seq", 0, 4)
    )
    top_score = jnp.maximum(global_max, self_score)
    factors = jnp.exp(global_max - top_score)
    den_sum = den_merged * factors
    acc_sum = acc_merged * factors[..., None]
    own_weight = jnp.exp(self_score - top_score)
    denominator = den_sum + own_weight
    numerator = acc_sum + own_weight[..., None] * new_values.reshape(
        batch_size, kv_local, 1, head_size
    ).astype(jnp.float32)
    mixed = (
        (numerator / denominator[..., None])
        .astype(jnp.bfloat16)
        .reshape(batch_size, kv_local * group_size * head_size)
    )
    output = summed_on_arrival(jnp.dot(mixed, w_out, preferred_element_type=jnp.float32), "head", 0)
    return output.astype(jnp.bfloat16)


def solution(mesh):
    return jax.shard_map(
        local,
        mesh=mesh,
        in_specs=(
            P(("parts", "head"), "seq"),
            P("seq"),
            P("seq", "head"),
            P("seq", "head"),
            P("seq", "head"),
            P("head", "seq"),
            P("parts"),
            P("parts", "head", "seq", None),
            P("parts", "head", "seq", None),
        ),
        out_specs=P(("parts", "head"), "seq"),
        check_vma=False,
    )
```

profile of v0, /device:TPU:33, one launch (start us, length us, event | category | flops | bytes accessed | tf_op | source)
XLA Modules:
  0.0 357.4 jit_solution(9531133762320092091)
XLA Ops:
  6.6 1.4 broadcast_in_dim.49
  8.0 44.7 %all-to-all-start = ((bf16[8,3,384]{2,1,0:T(4,128)(2,1)}), bf16[8,3,384]{2,1,0:T(4,128)(2,1)S(1)}, u32[]{:S(2)}, u32[]{:S(2)}) async-start(bf16[8,3,384]{2,1,0:T(4,128)(2,1)} %broadcast_in_dim.49), calls=%async_computation | async-start | bytes 49152 | tf_op jit(solution)/shard_map/all_to_all | solution.py:19
  52.7 1.7 copy.66
  54.4 3.0 all-to-all-done
  57.4 0.8 multiply_reduce_fusion
  58.9 6.8 %all-to-all-start.2 = ((f32[32,24,1]{1,2,0:T(1,128)}), f32[32,24,1]{1,2,0:T(1,128)S(1)}, u32[]{:S(2)}, u32[]{:S(2)}) async-start(f32[32,24,1]{1,2,0:T(1,128)} %transpose.24), calls=%async_computation.2 | async-start | bytes 32768 | tf_op jit(solution)/shard_map/all_to_all | solution.py:33
  66.3 1.6 convolution_bitcast_fusion
  67.8 1.1 reshape.206
  68.9 17.3 %all-to-all-done.2 = f32[32,24,1]{1,2,0:T(1,128)S(1)} async-done(((f32[32,24,1]{1,2,0:T(1,128)}), f32[32,24,1]{1,2,0:T(1,128)S(1)}, u32[]{:S(2)}, u32[]{:S(2)}) %all-to-all-start.2) | async-done | bytes 3104 | tf_op jit(solution)/shard_map/all_to_all | solution.py:33
  86.2 4.8 %all-to-all-start.1 = ((f32[32,1,1152]{2,1,0:T(1,128)}), f32[32,1,1152]{2,1,0:T(1,128)S(1)}, u32[]{:S(2)}, u32[]{:S(2)}) async-start(f32[32,1,1152]{2,1,0:T(1,128)} %reshape.206), calls=%async_computation.1 | async-start | bytes 294912 | tf_op jit(solution)/shard_map/all_to_all | solution.py:33
  91.9 27.9 %all-to-all-done.1 = f32[32,1,1152]{2,1,0:T(1,128)S(1)} async-done(((f32[32,1,1152]{2,1,0:T(1,128)}), f32[32,1,1152]{2,1,0:T(1,128)S(1)}, u32[]{:S(2)}, u32[]{:S(2)}) %all-to-all-start.1) | async-done | bytes 147488 | tf_op jit(solution)/shard_map/all_to_all | solution.py:33
  120.3 1.0 reduce.10
  121.7 38.6 %all-gather = bf16[32,48,24]{1,2,0:T(8,128)(2,1)S(1)} all-gather(bf16[1,48,24]{1,2,0:T(8,128)(2,1)S(1)} %fusion.13), channel_id=1, replica_groups=mesh['parts'=2,'seq'=32,'head'=8] {'seq'}, dimensions={0}, use_global_device_ids=true | all-gather | bytes 76032 | tf_op jit(solution)/shard_map/all_gather | solution.py:98
  162.7 0.9 copy.72
  163.6 1.0 fusion.14
  164.7 1.0 fusion.15
  166.0 30.1 %all_to_all.25 = f32[32,1,192]{2,1,0:T(1,128)S(1)} all-to-all(f32[32,1,192]{2,1,0:T(1,128)S(1)} %reshape.208), channel_id=1, replica_groups=mesh['parts'=2,'seq'=32,'head'=8] {'seq'}, dimensions={0} | all-to-all | bytes 49152 | tf_op jit(solution)/shard_map/all_to_all | solution.py:33
  197.1 42.9 %all-gather.1 = bf16[32,4,48]{2,1,0:T(4,128)(2,1)S(1)} all-gather(bf16[1,4,48]{2,1,0:T(4,128)(2,1)S(1)} %maximum_bitcast_fusion), channel_id=1, replica_groups=mesh['parts'=2,'seq'=32,'head'=8] {'seq'}, dimensions={0}, use_global_device_ids=true | all-gather | bytes 12672 | tf_op jit(solution)/shard_map/all_gather | solution.py:52
  240.4 61.3 %all-gather.4.cloned.1.call-done = f32[32,24,1,12,130]{4,1,3,2,0:T(8,128)} async-done(((f32[1,24,1,12,130]{4,1,3,2,0:T(8,128)}), f32[32,24,1,12,130]{4,1,3,2,0:T(8,128)}) %all-gather.4.cloned.1.call-update) | async-done | bytes 4792336 | tf_op jit(solution)/shard_map/all_gather | solution.py:60
  301.7 9.1 %fusion.18 = (f32[32,24,1,12,1]{4,1,3,2,0:T(8,128)}, f32[24,12]{0,1:T(8,128)S(1)}, f32[32,24,1,12,1]{4,1,3,2,0:T(8,128)}) fusion(f32[32,24,1,12,130]{4,1,3,2,0:T(8,128)} %all-gather.4.cloned.1.call-done), kind=kLoop, calls=%fused_computation.45 | loop fusion | flops 8928 | bytes 148608 | tf_op jit(solution)/shard_map/split | solution.py:61
  310.8 3.5 copy.88
  314.3 3.5 copy.87
  318.4 5.1 %fusion = f32[24,12,128]{2,0,1:T(8,128)S(1)} fusion(f32[32,24,1,12,130]{4,1,3,2,0:T(8,128)} %all-gather.4.cloned.1.call-done, f32[32,24,12]{1,2,0:T(8,128)S(1)} %copy.74), kind=kLoop, calls=%fused_computation.1 | loop fusion | flops 2322432 | bytes 4902912 | tf_op jit(solution)/shard_map/reduce_sum | solution.py:71
  324.0 25.8 %all_to_all.26 = f32[8,3,384]{2,1,0:T(4,128)S(1)} all-to-all(f32[8,3,384]{2,1,0:T(4,128)S(1)} %copy.80), channel_id=1, replica_groups=mesh['parts'=2,'seq'=32,'head'=8] {'head'}, dimensions={0} | all-to-all | bytes 73728 | tf_op jit(solution)/shard_map/all_to_all | solution.py:33
  (56 shorter events, 8.7 us)
Async XLA Ops:
  6.5 317.2 %copy-start = (bf16[1536,384]{1,0:T(8,128)(2,1)S(1)}, bf16[1536,384]{1,0:T(8,128)(2,1)}, u32[]{:S(2)}) copy-start(bf16[1536,384]{1,0:T(8,128)(2,1)} %param.14) | copy-start | bytes 3538948
  6.6 154.1 %copy-start.1 = (bf16[24,1,128,128]{3,2,1,0:T(8,128)(2,1)S(1)}, bf16[24,1,128,128]{3,2,1,0:T(8,128)(2,1)}, u32[]{:S(2)}) copy-start(bf16[24,1,128,128]{3,2,1,0:T(8,128)(2,1)} %param.16) | copy-start | bytes 2359300
  8.0 49.4 %all-to-all-start = ((bf16[8,3,384]{2,1,0:T(4,128)(2,1)}), bf16[8,3,384]{2,1,0:T(4,128)(2,1)S(1)}, u32[]{:S(2)}, u32[]{:S(2)}) async-start(bf16[8,3,384]{2,1,0:T(4,128)(2,1)} %broadcast_in_dim.49), calls=%async_computation | async-start | bytes 49152 | tf_op jit(solution)/shard_map/all_to_all | solution.py:19
  57.4 8.9 %copy-start.3 = (bf16[8,3,384]{2,1,0:T(4,128)(2,1)}, bf16[8,3,384]{2,1,0:T(4,128)(2,1)S(1)}, u32[]{:S(2)}) copy-start(bf16[8,3,384]{2,1,0:T(4,128)(2,1)S(1)} %all-to-all-done) | copy-start | bytes 55300
  58.9 27.3 %all-to-all-start.2 = ((f32[32,24,1]{1,2,0:T(1,128)}), f32[32,24,1]{1,2,0:T(1,128)S(1)}, u32[]{:S(2)}, u32[]{:S(2)}) async-start(f32[32,24,1]{1,2,0:T(1,128)} %transpose.24), calls=%async_computation.2 | async-start | bytes 32768 | tf_op jit(solution)/shard_map/all_to_all | solution.py:33
  67.8 93.6 %copy-start.2 = (bf16[24,1,128,128]{3,2,1,0:T(8,128)(2,1)S(1)}, bf16[24,1,128,128]{3,2,1,0:T(8,128)(2,1)}, u32[]{:S(2)}) copy-start(bf16[24,1,128,128]{3,2,1,0:T(8,128)(2,1)} %param.17) | copy-start | bytes 2359300
  68.9 94.7 %copy-start.4 = (bf16[8,3,384]{2,1,0:T(4,128)(2,1)S(1)}, bf16[8,3,384]{2,1,0:T(4,128)(2,1)}, u32[]{:S(2)}) copy-start(bf16[8,3,384]{2,1,0:T(4,128)(2,1)} %copy-done.3) | copy-start | bytes 55300
  86.2 33.6 %all-to-all-start.1 = ((f32[32,1,1152]{2,1,0:T(1,128)}), f32[32,1,1152]{2,1,0:T(1,128)S(1)}, u32[]{:S(2)}, u32[]{:S(2)}) async-start(f32[32,1,1152]{2,1,0:T(1,128)} %reshape.206), calls=%async_computation.1 | async-start | bytes 294912 | tf_op jit(solution)/shard_map/all_to_all | solution.py:33
  91.0 210.7 %all-gather.4.cloned.1.call-start = ((), (), s32[]{:S(2)}) async-start(), calls=%async_computation.5 | async-start | bytes 9732096 | tf_op jit(solution)/shard_map/all_gather | solution.py:60
Sparse Core Ops, SparseCore 0:
  163.7 137.9 all-gather.3
where the time goes:
time: 358 us; the launch traced here: 357 us
  blocking collectives  137 us (38%)
  waiting for transfers between devices  110 us (31%)
  starting transfers between devices  56.3 us (16%)
  other arithmetic  19.4 us (5%)
  local copies, waits for them, and re-layouts  15.8 us (4%)
  between operations  13.7 us (4%)
  matrix products  5.05 us (1%)
    all_gather x1, waiting for transfers between devices, side_by_side(): result = lax.all_gather(both, axis, axis=dim, tiled=True)  61.3 us
    all_to_all x2, blocking collectives, summed_on_arrival(): lax.all_to_all(tiles, axis, split_axis=0, concat_axis=0, tiled=True)  56 us
    all_to_all x2, waiting for transfers between devices, summed_on_arrival(): lax.all_to_all(tiles, axis, split_axis=0, concat_axis=0, tiled=True)  45.3 us
    all_to_all x1, starting transfers between devices, sent_to_all(): return lax.all_to_all(copies, axis, split_axis=0, concat_axis=0, tiled=True)  44.7 us
    all_gather x1, blocking collectives, in_one_piece_2(): lax.all_gather(both, axis, axis=dim, tiled=True)  42.9 us
    all_gather x1, blocking collectives, local(): lax.all_gather(queries, 'seq', axis=1, tiled=True)  38.6 us
    all_to_all x2, starting transfers between devices, summed_on_arrival(): lax.all_to_all(tiles, axis, split_axis=0, concat_axis=0, tiled=True)  11.5 us
    unnamed x19, local copies, waits for them, and re-layouts  10.6 us
  transfers between devices with their start and end apart: 4, of which 4 were waited for; matrix products, arithmetic and copies ran while one was open for 3% of the time, Pallas kernels for 0%

commit v1 on v0

--- a/solution.py
+++ b/solution.py
@@ -6,6 +6,11 @@
 
 D = 12288
 EPSILON = 1e-05
+
+
+def all_by_exchange(block, name, along):
+    outgoing = jnp.stack([block] * lax.axis_size(name))
+    return jnp.concatenate(lax.all_to_all(outgoing, name, 0, 0), axis=along)
 
 
 def in_order(tiles, dim):
@@ -95,7 +100,7 @@
     new_keys = (key_sum * inverse_rms).astype(jnp.bfloat16)
     new_values = (value_sum * inverse_rms).astype(jnp.bfloat16)
     queries, new_keys, new_values = (
-        lax.all_gather(queries, "seq", axis=1, tiled=True),
+        all_by_exchange(queries, "seq", 1),
         *in_one_piece_2((new_keys, new_values), "seq", 1, 0),
     )
     grouped = queries.reshape(batch_size, kv_local, group_size, head_size)

time: 358 us -> 332 us (0.927)
  blocking collectives: 137 us -> 92.8 us
  waiting for transfers between devices: 110 us -> 122 us
  starting transfers between devices: 56.3 us -> 62.1 us
    all_gather x1 -> x0, blocking collectives: 38.6 us -> none  [local(): lax.all_gather(queries, 'seq', axis=1, tiled=True)]
    all_to_all x0 -> x1, waiting for transfers between devices: none -> 22.5 us  [all_by_exchange(): return jnp.concatenate(lax.all_to_all(outgoing, name, 0, 0), axis=along)]
    all_gather x1, waiting for transfers between devices: 61.3 us -> 50.7 us  [side_by_side(): result = lax.all_gather(both, axis, axis=dim, tiled=True)]
    all_to_all x0 -> x1, starting transfers between devices: none -> 5.86 us  [all_by_exchange(): return jnp.concatenate(lax.all_to_all(outgoing, name, 0, 0), axis=along)]
    all_to_all x2, blocking collectives: 56 us -> 50.5 us  [summed_on_arrival(): lax.all_to_all(tiles, axis, split_axis=0, concat_axis=0, tiled=True)]
    unnamed x19 -> x24, local copies, waits for them, and re-layouts: 10.6 us -> 11.4 us
  transfers between devices with their start and end apart: 4 -> 5, of which waited for: 4 -> 5; matrix products, arithmetic and copies ran while one was open for 3% -> 3% of each run, Pallas kernels for 0% -> 0%
where the time goes in v1:
time: 332 us; the launch traced here: 331 us
  waiting for transfers between devices  122 us (37%)
  blocking collectives  92.8 us (28%)
  starting transfers between devices  62.1 us (19%)
  other arithmetic  19.4 us (6%)
  local copies, waits for them, and re-layouts  16.8 us (5%)
  between operations  13.7 us (4%)
  matrix products  4.13 us (1%)
    all_gather x1, waiting for transfers between devices, side_by_side(): result = lax.all_gather(both, axis, axis=dim, tiled=True)  50.7 us
    all_to_all x2, blocking collectives, summed_on_arrival(): lax.all_to_all(tiles, axis, split_axis=0, concat_axis=0, tiled=True)  50.5 us
    all_to_all x2, waiting for transfers between devices, summed_on_arrival(): lax.all_to_all(tiles, axis, split_axis=0, concat_axis=0, tiled=True)  46.1 us
    all_to_all x1, starting transfers between devices, sent_to_all(): return lax.all_to_all(copies, axis, split_axis=0, concat_axis=0, tiled=True)  44.7 us
    all_gather x1, blocking collectives, in_one_piece_2(): lax.all_gather(both, axis, axis=dim, tiled=True)  42.3 us
    all_to_all x1, waiting for transfers between devices, all_by_exchange(): return jnp.concatenate(lax.all_to_all(outgoing, name, 0, 0), axis=along)  22.5 us
    all_to_all x2, starting transfers between devices, summed_on_arrival(): lax.all_to_all(tiles, axis, split_axis=0, concat_axis=0, tiled=True)  11.5 us
    unnamed x24, local copies, waits for them, and re-layouts  11.4 us
  transfers between devices with their start and end apart: 5, of which 5 were waited for; matrix products, arithmetic and copies ran while one was open for 3% of the time, Pallas kernels for 0%

profile of v1, /device:TPU:33, one launch (start us, length us, event | category | flops | bytes accessed | tf_op | source)
XLA Modules:
  0.0 331.3 jit_solution(8045730332291931779)
XLA Ops:
  6.6 1.4 broadcast_in_dim.49
  8.0 44.7 %all-to-all-start = ((bf16[8,3,384]{2,1,0:T(4,128)(2,1)}), bf16[8,3,384]{2,1,0:T(4,128)(2,1)S(1)}, u32[]{:S(2)}, u32[]{:S(2)}) async-start(bf16[8,3,384]{2,1,0:T(4,128)(2,1)} %broadcast_in_dim.49), calls=%async_computation | async-start | bytes 49152 | tf_op jit(solution)/shard_map/all_to_all | solution.py:24
  52.7 1.7 copy.65
  54.4 3.0 all-to-all-done
  58.9 6.8 %all-to-all-start.2 = ((f32[32,24,1]{1,2,0:T(1,128)}), f32[32,24,1]{1,2,0:T(1,128)S(1)}, u32[]{:S(2)}, u32[]{:S(2)}) async-start(f32[32,24,1]{1,2,0:T(1,128)} %transpose.24), calls=%async_computation.2 | async-start | bytes 32768 | tf_op jit(solution)/shard_map/all_to_all | solution.py:38
  66.3 1.6 convolution_bitcast_fusion
  67.8 1.1 reshape.215
  68.9 17.3 %all-to-all-done.2 = f32[32,24,1]{1,2,0:T(1,128)S(1)} async-done(((f32[32,24,1]{1,2,0:T(1,128)}), f32[32,24,1]{1,2,0:T(1,128)S(1)}, u32[]{:S(2)}, u32[]{:S(2)}) %all-to-all-start.2) | async-done | bytes 3104 | tf_op jit(solution)/shard_map/all_to_all | solution.py:38
  86.2 4.8 %all-to-all-start.1 = ((f32[32,1,1152]{2,1,0:T(1,128)}), f32[32,1,1152]{2,1,0:T(1,128)S(1)}, u32[]{:S(2)}, u32[]{:S(2)}) async-start(f32[32,1,1152]{2,1,0:T(1,128)} %reshape.215), calls=%async_computation.1 | async-start | bytes 294912 | tf_op jit(solution)/shard_map/all_to_all | solution.py:38
  91.1 28.7 %all-to-all-done.1 = f32[32,1,1152]{2,1,0:T(1,128)S(1)} async-done(((f32[32,1,1152]{2,1,0:T(1,128)}), f32[32,1,1152]{2,1,0:T(1,128)S(1)}, u32[]{:S(2)}, u32[]{:S(2)}) %all-to-all-start.1) | async-done | bytes 147488 | tf_op jit(solution)/shard_map/all_to_all | solution.py:38
  120.3 1.0 reduce.10
  121.7 0.9 reshape.217
  122.6 5.9 %all-to-all-start.3 = ((bf16[32,2,576]{2,1,0:T(2,128)(2,1)}), bf16[32,2,576]{2,1,0:T(2,128)(2,1)S(1)}, u32[]{:S(2)}, u32[]{:S(2)}) async-start(bf16[32,2,576]{2,1,0:T(2,128)(2,1)} %reshape.217), calls=%async_computation.3 | async-start | bytes 163840 | tf_op jit(solution)/shard_map/all_to_all | solution.py:13
  129.3 22.5 %all-to-all-done.3 = bf16[32,2,576]{2,1,0:T(2,128)(2,1)S(1)} async-done(((bf16[32,2,576]{2,1,0:T(2,128)(2,1)}), bf16[32,2,576]{2,1,0:T(2,128)(2,1)S(1)}, u32[]{:S(2)}, u32[]{:S(2)}) %all-to-all-start.3) | async-done | bytes 73760 | tf_op jit(solution)/shard_map/all_to_all | solution.py:13
  154.3 0.9 copy.71
  155.5 1.0 fusion.14
  156.7 25.1 %all_to_all.30 = f32[32,1,192]{2,1,0:T(1,128)S(1)} all-to-all(f32[32,1,192]{2,1,0:T(1,128)S(1)} %reshape.219), channel_id=1, replica_groups=mesh['parts'=2,'seq'=32,'head'=8] {'seq'}, dimensions={0} | all-to-all | bytes 49152 | tf_op jit(solution)/shard_map/all_to_all | solution.py:38
  182.8 42.3 %all-gather = bf16[32,4,48]{2,1,0:T(4,128)(2,1)S(1)} all-gather(bf16[1,4,48]{2,1,0:T(4,128)(2,1)S(1)} %maximum_bitcast_fusion), channel_id=1, replica_groups=mesh['parts'=2,'seq'=32,'head'=8] {'seq'}, dimensions={0}, use_global_device_ids=true | all-gather | bytes 12672 | tf_op jit(solution)/shard_map/all_gather | solution.py:57
  225.5 50.7 %all-gather.3.cloned.1.call-done = f32[32,24,1,12,130]{4,1,3,2,0:T(8,128)} async-done(((f32[1,24,1,12,130]{4,1,3,2,0:T(8,128)}), f32[32,24,1,12,130]{4,1,3,2,0:T(8,128)}) %all-gather.3.cloned.1.call-update) | async-done | bytes 4792336 | tf_op jit(solution)/shard_map/all_gather | solution.py:65
  276.1 9.1 %fusion.17 = (f32[32,24,1,12,1]{4,1,3,2,0:T(8,128)}, f32[24,12]{0,1:T(8,128)S(1)}, f32[32,24,1,12,1]{4,1,3,2,0:T(8,128)}) fusion(f32[32,24,1,12,130]{4,1,3,2,0:T(8,128)} %all-gather.3.cloned.1.call-done), kind=kLoop, calls=%fused_computation.44 | loop fusion | flops 8928 | bytes 148608 | tf_op jit(solution)/shard_map/split | solution.py:66
  285.2 3.5 %copy.87 = f32[32,24,1,12,1]{0,1,4,3,2:T(8,128)S(1)} copy(f32[32,24,1,12,1]{4,1,3,2,0:T(8,128)} %get-tuple-element.8) | data formatting | bytes 73728
  288.7 3.5 %copy.86 = f32[32,24,1,12,1]{0,1,4,3,2:T(8,128)S(1)} copy(f32[32,24,1,12,1]{4,1,3,2,0:T(8,128)} %get-tuple-element.10) | data formatting | bytes 73728
  292.8 5.1 %fusion = f32[24,12,128]{2,0,1:T(8,128)S(1)} fusion(f32[32,24,1,12,130]{4,1,3,2,0:T(8,128)} %all-gather.3.cloned.1.call-done, f32[32,24,12]{1,2,0:T(8,128)S(1)} %copy.73), kind=kLoop, calls=%fused_computation.1 | loop fusion | flops 2322432 | bytes 4902912 | tf_op jit(solution)/shard_map/reduce_sum | solution.py:76
  298.4 25.4 %all_to_all.31 = f32[8,3,384]{2,1,0:T(4,128)S(1)} all-to-all(f32[8,3,384]{2,1,0:T(4,128)S(1)} %copy.79), channel_id=1, replica_groups=mesh['parts'=2,'seq'=32,'head'=8] {'head'}, dimensions={0} | all-to-all | bytes 73728 | tf_op jit(solution)/shard_map/all_to_all | solution.py:38
  (63 shorter events, 9.7 us)
Async XLA Ops:
  6.5 291.6 %copy-start = (bf16[1536,384]{1,0:T(8,128)(2,1)S(1)}, bf16[1536,384]{1,0:T(8,128)(2,1)}, u32[]{:S(2)}) copy-start(bf16[1536,384]{1,0:T(8,128)(2,1)} %param.14) | copy-start | bytes 3538948
  6.6 145.7 %copy-start.1 = (bf16[24,1,128,128]{3,2,1,0:T(8,128)(2,1)S(1)}, bf16[24,1,128,128]{3,2,1,0:T(8,128)(2,1)}, u32[]{:S(2)}) copy-start(bf16[24,1,128,128]{3,2,1,0:T(8,128)(2,1)} %param.16) | copy-start | bytes 2359300
  8.0 49.4 %all-to-all-start = ((bf16[8,3,384]{2,1,0:T(4,128)(2,1)}), bf16[8,3,384]{2,1,0:T(4,128)(2,1)S(1)}, u32[]{:S(2)}, u32[]{:S(2)}) async-start(bf16[8,3,384]{2,1,0:T(4,128)(2,1)} %broadcast_in_dim.49), calls=%async_computation | async-start | bytes 49152 | tf_op jit(solution)/shard_map/all_to_all | solution.py:24
  57.4 8.9 %copy-start.3 = (bf16[8,3,384]{2,1,0:T(4,128)(2,1)}, bf16[8,3,384]{2,1,0:T(4,128)(2,1)S(1)}, u32[]{:S(2)}) copy-start(bf16[8,3,384]{2,1,0:T(4,128)(2,1)S(1)} %all-to-all-done) | copy-start | bytes 55300
  58.9 27.3 %all-to-all-start.2 = ((f32[32,24,1]{1,2,0:T(1,128)}), f32[32,24,1]{1,2,0:T(1,128)S(1)}, u32[]{:S(2)}, u32[]{:S(2)}) async-start(f32[32,24,1]{1,2,0:T(1,128)} %transpose.24), calls=%async_computation.2 | async-start | bytes 32768 | tf_op jit(solution)/shard_map/all_to_all | solution.py:38
  67.8 85.3 %copy-start.2 = (bf16[24,1,128,128]{3,2,1,0:T(8,128)(2,1)S(1)}, bf16[24,1,128,128]{3,2,1,0:T(8,128)(2,1)}, u32[]{:S(2)}) copy-start(bf16[24,1,128,128]{3,2,1,0:T(8,128)(2,1)} %param.17) | copy-start | bytes 2359300
  68.9 86.4 %copy-start.4 = (bf16[8,3,384]{2,1,0:T(4,128)(2,1)S(1)}, bf16[8,3,384]{2,1,0:T(4,128)(2,1)}, u32[]{:S(2)}) copy-start(bf16[8,3,384]{2,1,0:T(4,128)(2,1)} %copy-done.3) | copy-start | bytes 55300
  68.9 86.4 %copy-start.5 = (bf16[384,128]{1,0:T(8,128)(2,1)S(1)}, bf16[384,128]{1,0:T(8,128)(2,1)}, u32[]{:S(2)}) copy-start(bf16[384,128]{1,0:T(8,128)(2,1)} %param.13) | copy-start | bytes 294916
  68.9 86.4 %copy-start.6 = (f32[384]{0:T(512)S(1)}, f32[384]{0:T(512)}, u32[]{:S(2)}) copy-start(f32[384]{0:T(512)} %param.10) | copy-start | bytes 4612
  86.2 33.6 %all-to-all-start.1 = ((f32[32,1,1152]{2,1,0:T(1,128)}), f32[32,1,1152]{2,1,0:T(1,128)S(1)}, u32[]{:S(2)}, u32[]{:S(2)}) async-start(f32[32,1,1152]{2,1,0:T(1,128)} %reshape.215), calls=%async_computation.1 | async-start | bytes 294912 | tf_op jit(solution)/shard_map/all_to_all | solution.py:38
  122.6 29.2 %all-to-all-start.3 = ((bf16[32,2,576]{2,1,0:T(2,128)(2,1)}), bf16[32,2,576]{2,1,0:T(2,128)(2,1)S(1)}, u32[]{:S(2)}, u32[]{:S(2)}) async-start(bf16[32,2,576]{2,1,0:T(2,128)(2,1)} %reshape.217), calls=%async_computation.3 | async-start | bytes 163840 | tf_op jit(solution)/shard_map/all_to_all | solution.py:13
  128.5 147.6 %all-gather.3.cloned.1.call-start = ((), (), s32[]{:S(2)}) async-start(), calls=%async_computation.6 | async-start | bytes 9732096 | tf_op jit(solution)/shard_map/all_gather | solution.py:65
Sparse Core Ops, SparseCore 0:
  155.4 120.6 all-gather.2
